TPU v7x, 128 devices: a whole 4x4x4 slice. The times are simulated.
128 devices in a mesh: gx: 4 (over z), gy: 32 (over x, y, core).
Axes of the slice: x: 4, y: 4, z: 4, core: 2. Of those that a mesh axis runs over, the one named last changes fastest.
Arguments:
- grid_state: bfloat16 [32768, 1024], P(('gx', 'gy')), may hold values from -6 to 6
- mesh_state: bfloat16 [32768, 1024], P(('gx', 'gy')), may hold values from -6 to 6
- encode_block: int32 [32768], P(('gx', 'gy')), may hold values from 0 to 255, as said below
- neighbour_block: int32 [256], P(('gx', 'gy')), may hold values from 0 to 255, as said below
- decode_block: int32 [32768], P(('gx', 'gy')), may hold values from 0 to 255, as said below
- encode_grid_gain: float32 [1024], replicated, may hold values from 0.25 to 1.75
- encode_mesh_gain: float32 [1024], replicated, may hold values from 0.25 to 1.75
- process_gain: float32 [1024], replicated, may hold values from 0.25 to 1.75
- decode_grid_gain: float32 [1024], replicated, may hold values from 0.25 to 1.75
- decode_mesh_gain: float32 [1024], replicated, may hold values from 0.25 to 1.75
- encode_query: bfloat16 [1024, 1024], replicated, may hold values from -0.1875 to 0.1875
- encode_keyval: bfloat16 [1024, 2048], replicated, may hold values from -0.1875 to 0.1875
- encode_out: bfloat16 [1024, 1024], replicated, may hold values from -0.1875 to 0.1875
- process_qkv: bfloat16 [1024, 3072], replicated, may hold values from -0.1875 to 0.1875
- process_out: bfloat16 [1024, 1024], replicated, may hold values from -0.1875 to 0.1875
- decode_query: bfloat16 [1024, 1024], replicated, may hold values from -0.1875 to 0.1875
- decode_keyval: bfloat16 [1024, 2048], replicated, may hold values from -0.1875 to 0.1875
- decode_out: bfloat16 [1024, 1024], replicated, may hold values from -0.1875 to 0.1875
Outputs:
- grid_update: bfloat16 [32768, 1024], P(('gx', 'gy'))
Inputs may be any that keep to these rules, and one draw needn't show every extreme that they name: `encode_block`: block b lies on the b // 2-th device of the order of mesh nodes. The grid points of one device name the blocks of one device at most 4 times in all; every block is named by some grid point; in every draw some device's blocks are named exactly 4 times by the grid points of every device. `neighbour_block`: never b itself, and at most two blocks away from b. `decode_block`: block b lies on the b // 2-th device. The grid points of one device name the blocks of one device at most 4 times in all; every block is named; in every draw some device's blocks are named exactly 4 times by the grid points of every device.
All inputs are finite; a program needn't handle non-finite values.
Results may differ from a plain program's by a relative error of at most 0.015.
Values may be sent and summed in bfloat16 or wider, within the bound.
A program may use at most 128 MiB of HBM per device.

v0:
```python
import functools

import jax
import jax.numpy as jnp
from jax import lax
from jax.experimental import pallas as pl
from jax.experimental.pallas import tpu as pltpu
from jax.sharding import PartitionSpec as P

HEADS = 16
BLOCK = 128
CAP = 4
DEVICES = 128
D = 1024
ROWS = 256
SLOTS = DEVICES * CAP
PAIR = 128
MASKED = -1e30
MESH = pl.DeviceIdType.MESH
BF = jnp.bfloat16
F32 = jnp.float32


def coordinates():
    gy = lax.axis_index("gy")
    return lax.axis_index("gx"), gy // 8, lax.rem(gy // 2, 4), lax.rem(gy, 2)


def device_at(z, x, y, c):
    return lax.rem(z + 4, 4), lax.rem(x + 4, 4) * 8 + lax.rem(y + 4, 4) * 2 + lax.rem(c + 2, 2)


def peer(k, sign):
    z, x, y, c = coordinates()
    return device_at(
        z + sign * lax.rem(k // 16, 4),
        x + sign * lax.rem(k, 4),
        y + sign * lax.rem(k // 4, 4),
        c + sign * (k // 64),
    )


def iota(shape, dim):
    return lax.broadcasted_iota(jnp.int32, shape, dim)


def ones_where(condition, dtype=BF):
    return jnp.where(condition, 1.0, 0.0).astype(dtype)


def matmul(a, b):
    return jnp.dot(a, b, preferred_element_type=F32)


def matmul_nt(a, b):
    return lax.dot_general(a, b, (((1,), (1,)), ((), ())), preferred_element_type=F32)


def norm_into(src, src_row, dst, dst_row, gain_ref, rows=ROWS):
    def step(i, carry):
        wide = src[pl.ds(pl.multiple_of(src_row + i * 32, 32), 32), :].astype(F32)
        scale = lax.rsqrt(jnp.mean(wide * wide, axis=-1, keepdims=True) + 1e-6)
        dst[pl.ds(pl.multiple_of(dst_row + i * 32, 32), 32), :] = (
            wide * scale * gain_ref[...]
        ).astype(BF)
        return carry

    lax.fori_loop(0, rows // 32, step, 0)


def project(a_ref, w_ref, columns, first_column, epilogue, tile=512):
    def step(n, carry):
        at = pl.multiple_of(n * tile, tile)
        out = matmul(a_ref[...], w_ref[:, pl.ds(pl.multiple_of(first_column + at, tile), tile)])
        epilogue(pl.ds(at, tile), out)
        return carry

    lax.fori_loop(0, columns // tile, step, 0)


def slot_plan(blocks):
    z, x, y, c = coordinates()
    owner = blocks >> 1
    k = (
        (((owner >> 3) & 3) - x & 3)
        + 4 * (((owner >> 1) & 3) - y & 3)
        + 16 * ((owner >> 5) - z & 3)
        + 64 * ((owner & 1) - c & 1)
    )
    matches = ones_where(iota((DEVICES, ROWS), 0) == k)
    earlier = ones_where(iota((ROWS, ROWS), 0) < iota((ROWS, ROWS), 1))
    counts = matmul(matches, earlier)
    rank = jnp.sum(matches.astype(F32) * counts, axis=0, keepdims=True).astype(jnp.int32)
    return matches, rank, k * CAP + rank


def label_table(matches, rank, blocks, base):
    coded = jnp.where(iota((PAIR, ROWS), 0) == rank + base, (blocks & 1) + 1, 0)
    return matmul_nt(matches, coded.astype(F32).astype(BF))


def interleave():
    m = iota((256, 256), 0)
    return ones_where(iota((256, 256), 1) == 64 * ((m >> 2) & 3) + 4 * (m >> 4) + (m & 3))


def separate():
    n = iota((256, 256), 0)
    return ones_where(iota((256, 256), 1) == 16 * ((n >> 2) & 15) + 4 * (n >> 6) + (n & 3))


def store_slabs(dst, j, rows, mix):
    tall = jnp.concatenate([rows[:, 256 * q : 256 * q + 256] for q in range(4)], axis=0)
    dst[pl.ds(16 * j, 16)] = matmul(mix, tall).astype(BF).reshape(16, 16, 256)


def load_slabs(src, j, unmix):
    tall = matmul(unmix, src[pl.ds(16 * j, 16)].reshape(256, 256)).astype(BF)
    return jnp.concatenate([tall[64 * q : 64 * q + 64] for q in range(4)], axis=1)


def pack(rows_ref, slot, dst, mix):
    def step(j, carry):
        chosen = ones_where(iota((64, ROWS), 0) + 64 * j == slot)
        store_slabs(dst, j, matmul(chosen, rows_ref[...]).astype(BF), mix)
        return carry

    lax.fori_loop(0, 8, step, 0)


def unpack(src, dst, unmix):
    def step(j, carry):
        dst[pl.ds(pl.multiple_of(64 * j, 64), 64), :] = load_slabs(src, j, unmix)
        return carry

    lax.fori_loop(0, 8, step, 0)


def attend_pair(queries, keys, values, bias):
    lane = iota((1, PAIR), 1)
    widened = jnp.concatenate([values, jnp.ones_like(values)], axis=1)
    outs = []
    for half in range(2):
        scores = matmul_nt(queries * ones_where((lane >= 64) == (half == 1)), keys)
        if bias is not None:
            scores = scores + bias
        powers = jnp.exp(scores - jnp.max(scores, axis=-1, keepdims=True)).astype(BF)
        both = matmul(powers, widened)
        outs.append(both[:, :PAIR] / both[:, PAIR:])
    return jnp.where(lane < 64, outs[0], outs[1]).astype(BF)


def kernel(
    grid_hbm, mesh_hbm, encode_block, decode_block, neighbour_block,
    encode_grid_gain, encode_mesh_gain, process_gain, decode_grid_gain, decode_mesh_gain,
    eq_hbm, ekv_hbm, eo_hbm, pqkv_hbm, po_hbm, dq_hbm, dkv_hbm, do_hbm,
    out_ref,
    grid, mesh, eq, ekv, eo, pqkv, po, dq, dkv, do,
    send1, recv1, send2, recv2, send3, recv3, lab2d, lab_send, lab_recv,
    rows_a, rows_b, query, mid, cand, wide_rows, keyval, bias_e, bias_d,
    load_sems, send_sems, recv_sems, halo_sems,
):
    z, x, y, c = coordinates()
    me = lax.axis_index("gx") * 32 + lax.axis_index("gy")
    barrier = pltpu.get_barrier_semaphore()

    def greet(k, carry):
        pl.semaphore_signal(barrier, inc=1, device_id=peer(k, 1), device_id_type=MESH)
        return carry

    loads = [
        pltpu.make_async_copy(src, dst, load_sems.at[i])
        for i, (src, dst) in enumerate(
            (
                (grid_hbm, grid), (dq_hbm, dq), (mesh_hbm, mesh), (eq_hbm, eq), (ekv_hbm, ekv),
                (eo_hbm, eo), (pqkv_hbm, pqkv), (po_hbm, po), (dkv_hbm, dkv), (do_hbm, do),
            )
        )
    ]
    loads[0].start()
    lax.fori_loop(1, DEVICES, greet, 0)
    for load in loads[1:]:
        load.start()

    mix = interleave()
    e_matches, e_rank, e_slot = slot_plan(encode_block[...])
    d_matches, d_rank, d_slot = slot_plan(decode_block[...])
    lab2d[...] = label_table(e_matches, e_rank, encode_block[...], 0) + label_table(
        d_matches, d_rank, decode_block[...], CAP
    )

    def spread(k, carry):
        lab_send[k] = lab2d[pl.ds(k, 1), :]
        return carry

    lax.fori_loop(0, DEVICES, spread, 0)
    loads[0].wait()
    norm_into(grid, 0, rows_a, 0, encode_grid_gain)
    pack(rows_a, e_slot, send1, mix)
    pl.semaphore_wait(barrier, DEVICES - 1)

    def remote(src, dst, which, k, sign):
        return pltpu.make_async_remote_copy(
            src_ref=src.at[k], dst_ref=dst.at[k], send_sem=send_sems.at[which],
            recv_sem=recv_sems.at[which], device_id=peer(k, sign), device_id_type=MESH,
        )

    def send_first(k, carry):
        remote(send1, recv1, 0, k, 1).start()
        remote(lab_send, lab_recv, 1, k, 1).start()
        return carry

    lax.fori_loop(1, DEVICES, send_first, 0)

    loads[1].wait()
    norm_into(grid, 0, rows_a, 0, decode_grid_gain)

    def store_query(at, out):
        rows_b[:, at] = (out * 0.125).astype(BF)

    project(rows_a, dq, D, 0, store_query)
    pack(rows_b, d_slot, send2, mix)

    def send_second(k, carry):
        remote(send2, recv2, 2, k, 1).start()
        return carry

    lax.fori_loop(1, DEVICES, send_second, 0)

    def all_slabs(ref):
        return ref.at[pl.ds(1, DEVICES - 1)]

    def wait_for(ref, sem):
        view = all_slabs(ref)
        pltpu.make_async_copy(view, view, sem).wait()

    loads[2].wait()
    norm_into(mesh, 0, rows_a, 0, encode_mesh_gain)
    loads[3].wait()

    def store_mesh_query(at, out):
        query[:, at] = (out * 0.125).astype(BF)

    project(rows_a, eq, D, 0, store_mesh_query)
    unmix = separate()
    recv1[0] = send1[0]
    recv2[0] = send2[0]
    lab_recv[0] = lab_send[0]
    loads[4].wait()
    wait_for(recv1, recv_sems.at[0])
    unpack(recv1, wide_rows, unmix)

    def store_keyval(at, out):
        keyval[:, at] = out.astype(BF)

    project(wide_rows, ekv, 2 * D, 0, store_keyval)

    wait_for(lab_recv, recv_sems.at[1])

    def gather_labels(k, carry):
        lab2d[pl.ds(k, 1), :] = lab_recv[k]
        return carry

    lax.fori_loop(0, DEVICES, gather_labels, 0)
    table = lab2d[...].astype(BF)
    spread_lanes = matmul(table, ones_where(iota((PAIR, SLOTS), 0) == (iota((PAIR, SLOTS), 1) & 3)))
    key_label = jnp.sum(
        jnp.where(iota((DEVICES, SLOTS), 0) == (iota((DEVICES, SLOTS), 1) >> 2), spread_lanes, 0.0),
        axis=0,
        keepdims=True,
    )
    spread_rows = matmul(ones_where((iota((SLOTS, DEVICES), 0) >> 2) == iota((SLOTS, DEVICES), 1)), table)
    query_label = jnp.sum(
        jnp.where(
            iota((SLOTS, PAIR), 1) == CAP + (iota((SLOTS, PAIR), 0) & 3), spread_rows, 0.0
        ),
        axis=1,
        keepdims=True,
    )
    block_row = iota((8, SLOTS), 0).astype(F32)
    bias_e[...] = jnp.where(key_label == block_row + 1.0, 0.0, MASKED)
    key_block = (iota((SLOTS, ROWS), 1) >> 7).astype(F32)
    bias_d[...] = jnp.where(query_label == key_block + 1.0, 0.0, MASKED)

    def encode_pair(p, carry):
        at = pl.ds(pl.multiple_of(p * PAIR, PAIR), PAIR)
        upper = pl.ds(pl.multiple_of(D + p * PAIR, PAIR), PAIR)
        for block in range(2):
            here = pl.ds(block * BLOCK, BLOCK)
            rows_a[here, at] = attend_pair(
                query[here, at], keyval[:, at], keyval[:, upper], bias_e[pl.ds(block, 1), :]
            )
        return carry

    lax.fori_loop(0, HEADS // 2, encode_pair, 0)

    loads[5].wait()

    def store_mid(at, out):
        mid[:, at] = (mesh[:, at].astype(F32) + out).astype(BF)

    project(rows_a, eo, D, 0, store_mid)
    norm_into(mid, 0, cand, ROWS, process_gain)

    def neighbour(step, sem, to):
        there = lax.rem(me + step + DEVICES, DEVICES)
        return pltpu.make_async_remote_copy(
            src_ref=cand.at[pl.ds(ROWS, ROWS)], dst_ref=cand.at[pl.ds(to, ROWS)],
            send_sem=halo_sems.at[sem], recv_sem=halo_sems.at[sem + 1],
            device_id=(there // 32, lax.rem(there, 32)), device_id_type=MESH,
        )

    to_right = neighbour(1, 0, 0)
    to_left = neighbour(-1, 2, 2 * ROWS)
    to_right.start()
    to_left.start()

    loads[6].wait()

    def store_process_query(at, out):
        query[:, at] = (out * 0.125).astype(BF)

    def store_own(at, out):
        keyval[pl.ds(0, ROWS), at] = out.astype(BF)

    def store_other(at, out):
        keyval[pl.ds(ROWS, ROWS), at] = out.astype(BF)

    own = cand.at[pl.ds(ROWS, ROWS)]
    project(own, pqkv, D, 0, store_process_query)
    project(own, pqkv, 2 * D, D, store_own)
    to_right.wait()
    to_left.wait()
    for block in range(2):
        position = neighbour_block[pl.ds(block, 1), :] - 2 * me + 2
        picked = None
        for candidate in (block, block + 1, block + 3, block + 4):
            weight = ones_where(position == candidate)
            weight = jnp.concatenate([weight] * (D // PAIR), axis=1)
            term = cand[pl.ds(candidate * BLOCK, BLOCK), :] * weight
            picked = term if picked is None else picked + term
        rows_b[pl.ds(block * BLOCK, BLOCK), :] = picked
    project(rows_b, pqkv, 2 * D, D, store_other)

    def process_pair(p, carry):
        at = pl.ds(pl.multiple_of(p * PAIR, PAIR), PAIR)
        upper = pl.ds(pl.multiple_of(D + p * PAIR, PAIR), PAIR)
        for block in range(2):
            here = pl.ds(block * BLOCK, BLOCK)
            there = pl.ds(ROWS + block * BLOCK, BLOCK)
            rows_a[here, at] = attend_pair(
                query[here, at],
                jnp.concatenate([keyval[here, at], keyval[there, at]], axis=0),
                jnp.concatenate([keyval[here, upper], keyval[there, upper]], axis=0),
                None,
            )
        return carry

    lax.fori_loop(0, HEADS // 2, process_pair, 0)
    loads[7].wait()

    def store_mesh_out(at, out):
        rows_b[:, at] = (mid[:, at].astype(F32) + out).astype(BF)

    project(rows_a, po, D, 0, store_mesh_out)
    norm_into(rows_b, 0, rows_a, 0, decode_mesh_gain)
    loads[8].wait()
    project(rows_a, dkv, 2 * D, 0, store_own)

    wait_for(recv2, recv_sems.at[2])
    unpack(recv2, wide_rows, unmix)

    for chunk in range(4):
        here = pl.ds(chunk * BLOCK, BLOCK)

        def decode_pair(p, carry):
            at = pl.ds(pl.multiple_of(p * PAIR, PAIR), PAIR)
            upper = pl.ds(pl.multiple_of(D + p * PAIR, PAIR), PAIR)
            mine = pl.ds(0, ROWS)
            rows_a[pl.ds(0, BLOCK), at] = attend_pair(
                wide_rows[here, at], keyval[mine, at], keyval[mine, upper], bias_d[here, :]
            )
            return carry

        lax.fori_loop(0, HEADS // 2, decode_pair, 0)
        for j in range(2):
            store_slabs(send3, 2 * chunk + j, rows_a[pl.ds(64 * j, 64), :], mix)

        def send_third(k, carry):
            remote(send3, recv3, 3, k, -1).start()
            return carry

        lax.fori_loop(max(1, 32 * chunk), 32 * chunk + 32, send_third, 0)
    recv3[0] = send3[0]
    wait_for(send1, send_sems.at[0])
    wait_for(lab_send, send_sems.at[1])
    wait_for(send2, send_sems.at[2])
    wait_for(recv3, recv_sems.at[3])
    unpack(recv3, wide_rows, unmix)
    slot_column = jnp.sum(
        jnp.where(iota((ROWS, ROWS), 0) == iota((ROWS, ROWS), 1), d_slot, 0).astype(F32),
        axis=1,
        keepdims=True,
    )
    choose = ones_where(iota((ROWS, SLOTS), 1).astype(F32) == slot_column)
    rows_b[...] = matmul(choose, wide_rows[...]).astype(BF)
    loads[9].wait()

    def store_out(at, out):
        out_ref[:, at] = out.astype(BF)

    project(rows_b, do, D, 0, store_out)
    wait_for(send3, send_sems.at[3])


def on_device(
    grid_state, mesh_state, encode_block, neighbour_block, decode_block,
    encode_grid_gain, encode_mesh_gain, process_gain, decode_grid_gain, decode_mesh_gain,
    encode_query, encode_keyval, encode_out, process_qkv, process_out,
    decode_query, decode_keyval, decode_out,
):
    hbm = pl.BlockSpec(memory_space=pl.ANY)
    vmem = pl.BlockSpec(memory_space=pltpu.VMEM)
    slabs = pltpu.VMEM((DEVICES, 16, 256), BF)
    rows = pltpu.VMEM((ROWS, D), BF)
    return pl.pallas_call(
        kernel,
        out_shape=jax.ShapeDtypeStruct((ROWS, D), BF),
        in_specs=[hbm, hbm, vmem, vmem, vmem] + [vmem] * 5 + [hbm] * 8,
        out_specs=vmem,
        scratch_shapes=[
            rows, rows,
            pltpu.VMEM((D, D), BF), pltpu.VMEM((D, 2 * D), BF), pltpu.VMEM((D, D), BF),
            pltpu.VMEM((D, 3 * D), BF), pltpu.VMEM((D, D), BF), pltpu.VMEM((D, D), BF),
            pltpu.VMEM((D, 2 * D), BF), pltpu.VMEM((D, D), BF),
            slabs, slabs, slabs, slabs, slabs, slabs,
            pltpu.VMEM((DEVICES, PAIR), F32),
            pltpu.VMEM((DEVICES, 1, PAIR), F32), pltpu.VMEM((DEVICES, 1, PAIR), F32),
            rows, rows, rows, rows,
            pltpu.VMEM((3 * ROWS, D), BF), pltpu.VMEM((SLOTS, D), BF),
            pltpu.VMEM((SLOTS, 2 * D), BF),
            pltpu.VMEM((8, SLOTS), F32), pltpu.VMEM((SLOTS, ROWS), F32),
            pltpu.SemaphoreType.DMA((10,)), pltpu.SemaphoreType.DMA((4,)),
            pltpu.SemaphoreType.DMA((4,)), pltpu.SemaphoreType.DMA((4,)),
        ],
        compiler_params=pltpu.CompilerParams(
            collective_id=0, has_side_effects=True, vmem_limit_bytes=60 * 1024 * 1024
        ),
    )(
        grid_state, mesh_state, encode_block.reshape(1, -1), decode_block.reshape(1, -1),
        jnp.broadcast_to(neighbour_block[:, None], (2, PAIR)),
        *(
            gain.reshape(1, -1)
            for gain in (
                encode_grid_gain, encode_mesh_gain, process_gain, decode_grid_gain, decode_mesh_gain,
            )
        ),
        encode_query, encode_keyval, encode_out, process_qkv, process_out,
        decode_query, decode_keyval, decode_out,
    )


def solution(mesh):
    rows, split = P(("gx", "gy"), None), P(("gx", "gy"))
    return jax.shard_map(
        on_device,
        mesh=mesh,
        in_specs=(rows, rows, split, split, split) + (P(),) * 13,
        out_specs=rows,
        check_vma=False,
    )
```

profile of v0, /device:TPU:1, one launch (start us, length us, event | category | flops | bytes accessed | tf_op | source)
XLA Modules:
  0.0 98.0 jit_solution(9237007610601289510)
XLA Ops:
  0.0 1.3 %broadcast_in_dim.2.neighbour_block = s32[2,128]{1,0:T(2,128)} broadcast(s32[2]{0:T(128)} %param.21), dimensions={0} | broadcast | bytes 1032 | tf_op jit(solution)/shard_map/broadcast_in_dim | solution.py:451
  1.3 94.8 %shard_map.172 = bf16[256,1024]{1,0:T(8,128)(2,1)} custom-call(bf16[256,1024]{1,0:T(8,128)(2,1)} %grid_hbm.1, bf16[256,1024]{1,0:T(8,128)(2,1)} %mesh_hbm.1, s32[1,256]{1,0:T(1,128)} %bitcast.12, s32[1,256]{1,0:T(1,128)} %bitcast.13, s32[2,128]{1,0:T(2,128)} %broadcast_in_dim.2.neighbour_block, f32[1,1024]{1,0:T(1,128)} %bitcast.7, f32[1,1024]{1,0:T(1,128)} %bitcast.8, ...), custom_call_target="tpu_custom_call" | custom-call | tf_op jit(solution)/shard_map/pallas_call | solution.py:426
  96.1 1.9 %copy.20 = bf16[256,1024]{1,0:T(8,128)(2,1)} copy(bf16[256,1024]{1,0:T(8,128)(2,1)} %shard_map.172) | data formatting | bytes 1048576
where the time goes:
time: 98.2 us; the launch traced here: 98 us
  Pallas kernels  94.8 us (97%)
  local copies, waits for them, and re-layouts  3.15 us (3%)
    pallas_call x1, Pallas kernels, on_device(): pl.pallas_call(kernel, out_shape=jax.ShapeDtypeStruct((ROWS, D), BF), in_...  94.8 us

commit v1 on v0

v1 whole, which is shorter than its diff:
```python
import math

import jax
import jax.numpy as jnp
from jax import lax
from jax.experimental import pallas as pl
from jax.experimental.pallas import tpu as pltpu
from jax.sharding import PartitionSpec as P

HEADS = 16
BLOCK = 128
CAP = 4
DEVICES = 128
D = 1024
ROWS = 256
SLOTS = DEVICES * CAP
PAIR = 128
MASKED = -1e30
SCORE_SCALE = 0.125 * math.log2(math.e)
MESH = pl.DeviceIdType.MESH
BF = jnp.bfloat16
F32 = jnp.float32


def coordinates():
    gy = lax.axis_index("gy")
    return lax.axis_index("gx"), gy // 8, lax.rem(gy // 2, 4), lax.rem(gy, 2)


def device_at(z, x, y, c):
    return lax.rem(z + 4, 4), lax.rem(x + 4, 4) * 8 + lax.rem(y + 4, 4) * 2 + lax.rem(c + 2, 2)


def peer(k, sign):
    z, x, y, c = coordinates()
    return device_at(
        z + sign * lax.rem(k // 16, 4),
        x + sign * lax.rem(k, 4),
        y + sign * lax.rem(k // 4, 4),
        c + sign * (k // 64),
    )


def iota(shape, dim):
    return lax.broadcasted_iota(jnp.int32, shape, dim)


def ones_where(condition, dtype=BF):
    return jnp.where(condition, 1.0, 0.0).astype(dtype)


def matmul(a, b):
    return jnp.dot(a, b, preferred_element_type=F32)


def matmul_nt(a, b):
    return lax.dot_general(a, b, (((1,), (1,)), ((), ())), preferred_element_type=F32)


def norm_into(src, src_row, dst, dst_row, gain_ref, rows=ROWS):
    def step(i, carry):
        wide = src[pl.ds(pl.multiple_of(src_row + i * 32, 32), 32), :].astype(F32)
        scale = lax.rsqrt(jnp.mean(wide * wide, axis=-1, keepdims=True) + 1e-6)
        dst[pl.ds(pl.multiple_of(dst_row + i * 32, 32), 32), :] = (
            wide * scale * gain_ref[...]
        ).astype(BF)
        return carry

    lax.fori_loop(0, rows // 32, step, 0)


def project(a_ref, w_ref, columns, first_column, epilogue, tile=512):
    def step(n, carry):
        at = pl.multiple_of(n * tile, tile)
        out = matmul(a_ref[...], w_ref[:, pl.ds(pl.multiple_of(first_column + at, tile), tile)])
        epilogue(pl.ds(at, tile), out)
        return carry

    lax.fori_loop(0, columns // tile, step, 0)


def slot_plan(blocks):
    z, x, y, c = coordinates()
    owner = blocks >> 1
    k = (
        (((owner >> 3) & 3) - x & 3)
        + 4 * (((owner >> 1) & 3) - y & 3)
        + 16 * ((owner >> 5) - z & 3)
        + 64 * ((owner & 1) - c & 1)
    )
    matches = ones_where(iota((DEVICES, ROWS), 0) == k)
    earlier = ones_where(iota((ROWS, ROWS), 0) < iota((ROWS, ROWS), 1))
    counts = matmul(matches, earlier)
    rank = jnp.sum(matches.astype(F32) * counts, axis=0, keepdims=True).astype(jnp.int32)
    return matches, rank, k * CAP + rank


def label_table(matches, rank, blocks, base):
    coded = jnp.where(iota((PAIR, ROWS), 0) == rank + base, (blocks & 1) + 1, 0)
    return matmul_nt(matches, coded.astype(F32).astype(BF))


def interleave():
    m = iota((256, 256), 0)
    return ones_where(iota((256, 256), 1) == 64 * ((m >> 2) & 3) + 4 * (m >> 4) + (m & 3))


def separate():
    n = iota((256, 256), 0)
    return ones_where(iota((256, 256), 1) == 16 * ((n >> 2) & 15) + 4 * (n >> 6) + (n & 3))


def store_slabs(dst, j, rows, mix):
    tall = jnp.concatenate([rows[:, 256 * q : 256 * q + 256] for q in range(4)], axis=0)
    dst[pl.ds(16 * j, 16)] = matmul(mix, tall).astype(BF).reshape(16, 16, 256)


def load_slabs(src, j, unmix):
    tall = matmul(unmix, src[pl.ds(16 * j, 16)].reshape(256, 256)).astype(BF)
    return jnp.concatenate([tall[64 * q : 64 * q + 64] for q in range(4)], axis=1)


def pack(rows_ref, slot, dst, mix, first, last):
    def step(j, carry):
        chosen = ones_where(iota((64, ROWS), 0) + 64 * j == slot)
        store_slabs(dst, j, matmul(chosen, rows_ref[...]).astype(BF), mix)
        return carry

    lax.fori_loop(first, last, step, 0)


def unpack(src, dst, unmix, first, last):
    def step(j, carry):
        dst[pl.ds(pl.multiple_of(64 * j, 64), 64), :] = load_slabs(src, j, unmix)
        return carry

    lax.fori_loop(first, last, step, 0)


def attend_pairs(pairs):
    lane = iota((1, PAIR), 1)
    scores, outs = [], []
    for queries, query_tag, keys, key_tag, values in pairs:
        if key_tag is not None:
            keys = jnp.concatenate([keys, key_tag], axis=1)
        for half in range(2):
            part = queries * ones_where((lane >= 64) == (half == 1))
            if query_tag is not None:
                part = jnp.concatenate([part, query_tag], axis=1)
            scores.append(matmul_nt(part, keys))
    powers = [jnp.exp2(x - jnp.max(x, axis=-1, keepdims=True)).astype(BF) for x in scores]
    for i, (_, _, _, _, values) in enumerate(pairs):
        widened = jnp.concatenate([values, jnp.ones_like(values)], axis=1)
        halves = [matmul(powers[2 * i + half], widened) for half in range(2)]
        halves = [both[:, :PAIR] / both[:, PAIR:] for both in halves]
        outs.append(jnp.where(lane < 64, halves[0], halves[1]).astype(BF))
    return outs


def kernel(
    grid_hbm, mesh_hbm, encode_block, decode_block, neighbour_block,
    encode_grid_gain, encode_mesh_gain, process_gain, decode_grid_gain, decode_mesh_gain,
    eq_hbm, ekv_hbm, eo_hbm, pqkv_hbm, po_hbm, dq_hbm, dkv_hbm, do_hbm,
    out_ref,
    grid, mesh, eq, ekv, eo, pqkv, po, dq, dkv, do,
    send1, recv1, send2, recv2, send3, recv3, lab2d, lab_send, lab_recv,
    rows_a, rows_b, query, mid, cand, wide_rows, keyval, key_tags, query_tags,
    load_sems, send_sems, recv_sems, halo_sems,
):
    z, x, y, c = coordinates()
    me = lax.axis_index("gx") * 32 + lax.axis_index("gy")
    barrier = pltpu.get_barrier_semaphore()

    def greet(k, carry):
        pl.semaphore_signal(barrier, inc=1, device_id=peer(k, 1), device_id_type=MESH)
        return carry

    loads = [
        pltpu.make_async_copy(src, dst, load_sems.at[i])
        for i, (src, dst) in enumerate(
            (
                (grid_hbm, grid), (dq_hbm, dq), (mesh_hbm, mesh), (eq_hbm, eq), (ekv_hbm, ekv),
                (eo_hbm, eo), (pqkv_hbm, pqkv), (po_hbm, po), (dkv_hbm, dkv), (do_hbm, do),
            )
        )
    ]
    loads[0].start()
    lax.fori_loop(1, DEVICES, greet, 0)
    for load in loads[1:]:
        load.start()

    def remote(src, dst, sent, received, k, sign):
        return pltpu.make_async_remote_copy(
            src_ref=src.at[k], dst_ref=dst.at[k], send_sem=send_sems.at[sent],
            recv_sem=recv_sems.at[received], device_id=peer(k, sign), device_id_type=MESH,
        )

    def send_range(src, dst, sent, received, first, last, sign):
        def send(k, carry):
            remote(src, dst, sent, received, k, sign).start()
            return carry

        lax.fori_loop(max(1, first), last, send, 0)

    def wait_for(ref, first, last, sem):
        view = ref.at[pl.ds(max(1, first), last - max(1, first))]
        pltpu.make_async_copy(view, view, sem).wait()

    mix, unmix = interleave(), separate()
    e_matches, e_rank, e_slot = slot_plan(encode_block[...])
    loads[0].wait()
    norm_into(grid, 0, rows_a, 0, encode_grid_gain)
    pack(rows_a, e_slot, send1, mix, 0, 4)
    pl.semaphore_wait(barrier, DEVICES - 1)
    send_range(send1, recv1, 0, 0, 0, 64, 1)
    pack(rows_a, e_slot, send1, mix, 4, 8)
    send_range(send1, recv1, 0, 1, 64, 128, 1)

    d_matches, d_rank, d_slot = slot_plan(decode_block[...])
    lab2d[...] = label_table(e_matches, e_rank, encode_block[...], 0) + label_table(
        d_matches, d_rank, decode_block[...], CAP
    )

    def spread(k, carry):
        lab_send[k] = lab2d[pl.ds(k, 1), :]
        return carry

    lax.fori_loop(0, DEVICES, spread, 0)
    norm_into(grid, 0, rows_a, 0, decode_grid_gain)
    send_range(lab_send, lab_recv, 1, 2, 0, 128, 1)

    loads[1].wait()

    def store_query(at, out):
        rows_b[:, at] = (out * SCORE_SCALE).astype(BF)

    project(rows_a, dq, D, 0, store_query)
    pack(rows_b, d_slot, send2, mix, 0, 8)
    for group in range(2):
        send_range(send2, recv2, 2, 3 + group, 32 * group, 32 * group + 32, 1)

    loads[2].wait()
    norm_into(mesh, 0, rows_a, 0, encode_mesh_gain)
    loads[3].wait()

    def store_mesh_query(at, out):
        query[:, at] = (out * SCORE_SCALE).astype(BF)

    project(rows_a, eq, D, 0, store_mesh_query)
    recv1[0] = send1[0]
    recv2[0] = send2[0]
    lab_recv[0] = lab_send[0]
    loads[4].wait()
    for group in range(2):
        wait_for(recv1, 64 * group, 64 * group + 64, recv_sems.at[group])
        unpack(recv1, wide_rows, unmix, 4 * group, 4 * group + 4)
        part = pl.ds(group * ROWS, ROWS)

        def store_keyval(at, out):
            keyval[part, at] = out.astype(BF)

        project(wide_rows.at[part], ekv, 2 * D, 0, store_keyval)

    wait_for(lab_recv, 0, DEVICES, recv_sems.at[2])

    def gather_labels(k, carry):
        lab2d[pl.ds(k, 1), :] = lab_recv[k]
        return carry

    lax.fori_loop(0, DEVICES, gather_labels, 0)
    spread_rows = matmul(
        ones_where((iota((SLOTS, DEVICES), 0) >> 2) == iota((SLOTS, DEVICES), 1)),
        lab2d[...].astype(BF),
    )
    slot_lane = iota((SLOTS, PAIR), 1)
    slot_rank = iota((SLOTS, PAIR), 0) & 3

    def slot_tags(base):
        label = jnp.sum(
            jnp.where(slot_lane == base + slot_rank, spread_rows, 0.0), axis=1, keepdims=True
        )
        other = label != (slot_lane + 1).astype(F32)
        return jnp.where(other & (slot_lane < 2), MASKED, 0.0).astype(BF)

    key_tags[...] = slot_tags(0)
    query_tags[...] = slot_tags(CAP)

    def pair_at(p):
        return (
            pl.ds(pl.multiple_of(p * PAIR, PAIR), PAIR),
            pl.ds(pl.multiple_of(D + p * PAIR, PAIR), PAIR),
        )

    def halo(block, step, sem, to):
        there = lax.rem(me + step + DEVICES, DEVICES)
        return pltpu.make_async_remote_copy(
            src_ref=cand.at[pl.ds(ROWS + block * BLOCK, BLOCK)],
            dst_ref=cand.at[pl.ds(to + block * BLOCK, BLOCK)],
            send_sem=halo_sems.at[sem], recv_sem=halo_sems.at[sem + 1],
            device_id=(there // 32, lax.rem(there, 32)), device_id_type=MESH,
        )

    halos = []
    loads[5].wait()
    for block in range(2):
        here = pl.ds(block * BLOCK, BLOCK)
        block_tag = ones_where(iota((BLOCK, PAIR), 1) == block)

        def encode_pairs(g, carry):
            spots = [pair_at(4 * g + i) for i in range(4)]
            outs = attend_pairs(
                [
                    (query[here, at], block_tag, keyval[:, at], key_tags[...], keyval[:, upper])
                    for at, upper in spots
                ]
            )
            for (at, _), out in zip(spots, outs):
                rows_a[here, at] = out
            return carry

        lax.fori_loop(0, 2, encode_pairs, 0)

        def store_mid(at, out):
            mid[here, at] = (mesh[here, at].astype(F32) + out).astype(BF)

        project(rows_a.at[here], eo, D, 0, store_mid)
        norm_into(mid, block * BLOCK, cand, ROWS + block * BLOCK, process_gain, BLOCK)
        for step, sem, to in ((1, 4 * block, 0), (-1, 4 * block + 2, 2 * ROWS)):
            halos.append(halo(block, step, sem, to))
            halos[-1].start()
    for group in range(2, 4):
        send_range(send2, recv2, 2, 3 + group, 32 * group, 32 * group + 32, 1)

    loads[6].wait()

    def store_process_query(at, out):
        query[:, at] = (out * SCORE_SCALE).astype(BF)

    def store_own(at, out):
        keyval[pl.ds(0, ROWS), at] = out.astype(BF)

    def store_other(at, out):
        keyval[pl.ds(ROWS, ROWS), at] = out.astype(BF)

    own = cand.at[pl.ds(ROWS, ROWS)]
    project(own, pqkv, D, 0, store_process_query)
    project(own, pqkv, 2 * D, D, store_own)
    for copy in halos:
        copy.wait()
    for block in range(2):
        target = jnp.sum(
            jnp.where(iota((1, 2), 1) == block, neighbour_block[...], 0).astype(F32),
            axis=1,
            keepdims=True,
        )
        position = target - (2 * me - 2).astype(F32) + jnp.zeros((1, PAIR), F32)
        picked = None
        for candidate in (block, block + 1, block + 3, block + 4):
            weight = jnp.concatenate([ones_where(position == candidate)] * (D // PAIR), axis=1)
            term = cand[pl.ds(candidate * BLOCK, BLOCK), :] * weight
            picked = term if picked is None else picked + term
        rows_b[pl.ds(block * BLOCK, BLOCK), :] = picked
    project(rows_b, pqkv, 2 * D, D, store_other)

    def process_pairs(g, carry):
        spots = [(block, *pair_at(2 * g + i)) for i in range(2) for block in range(2)]
        work = []
        for block, at, upper in spots:
            here = pl.ds(block * BLOCK, BLOCK)
            there = pl.ds(ROWS + block * BLOCK, BLOCK)
            work.append(
                (
                    query[here, at], None,
                    jnp.concatenate([keyval[here, at], keyval[there, at]], axis=0), None,
                    jnp.concatenate([keyval[here, upper], keyval[there, upper]], axis=0),
                )
            )
        for (block, at, _), out in zip(spots, attend_pairs(work)):
            rows_a[pl.ds(block * BLOCK, BLOCK), at] = out
        return carry

    lax.fori_loop(0, HEADS // 4, process_pairs, 0)
    loads[7].wait()

    def store_mesh_out(at, out):
        rows_b[:, at] = (mid[:, at].astype(F32) + out).astype(BF)

    project(rows_a, po, D, 0, store_mesh_out)
    norm_into(rows_b, 0, rows_a, 0, decode_mesh_gain)
    loads[8].wait()
    project(rows_a, dkv, 2 * D, 0, store_own)

    node_tag = ones_where(iota((ROWS, PAIR), 1) == (iota((ROWS, PAIR), 0) >> 7))
    mine = pl.ds(0, ROWS)
    for chunk in range(4):
        here = pl.ds(chunk * BLOCK, BLOCK)
        wait_for(recv2, 32 * chunk, 32 * chunk + 32, recv_sems.at[3 + chunk])
        unpack(recv2, wide_rows, unmix, 2 * chunk, 2 * chunk + 2)

        def decode_pairs(g, carry):
            spots = [pair_at(4 * g + i) for i in range(4)]
            outs = attend_pairs(
                [
                    (
                        wide_rows[here, at], query_tags[here, :],
                        keyval[mine, at], node_tag, keyval[mine, upper],
                    )
                    for at, upper in spots
                ]
            )
            for (at, _), out in zip(spots, outs):
                rows_a[pl.ds(0, BLOCK), at] = out
            return carry

        lax.fori_loop(0, 2, decode_pairs, 0)
        for j in range(2):
            store_slabs(send3, 2 * chunk + j, rows_a[pl.ds(64 * j, 64), :], mix)
        send_range(send3, recv3, 3, 7 + chunk, 32 * chunk, 32 * chunk + 32, -1)
    recv3[0] = send3[0]
    slot_column = jnp.sum(
        jnp.where(iota((ROWS, ROWS), 0) == iota((ROWS, ROWS), 1), d_slot, 0).astype(F32),
        axis=1,
        keepdims=True,
    )
    wait_for(send1, 0, DEVICES, send_sems.at[0])
    wait_for(lab_send, 0, DEVICES, send_sems.at[1])
    wait_for(send2, 0, DEVICES, send_sems.at[2])
    decoded = None
    for chunk in range(4):
        choose = ones_where(
            (iota((ROWS, BLOCK), 1) + chunk * BLOCK).astype(F32) == slot_column
        )
        wait_for(recv3, 32 * chunk, 32 * chunk + 32, recv_sems.at[7 + chunk])
        unpack(recv3, wide_rows, unmix, 2 * chunk, 2 * chunk + 2)
        found = matmul(choose, wide_rows[pl.ds(chunk * BLOCK, BLOCK), :])
        decoded = found if decoded is None else decoded + found
    rows_b[...] = decoded.astype(BF)
    loads[9].wait()

    def store_out(at, out):
        out_ref[:, at] = out.astype(BF)

    project(rows_b, do, D, 0, store_out)
    wait_for(send3, 0, DEVICES, send_sems.at[3])


def on_device(
    grid_state, mesh_state, encode_block, neighbour_block, decode_block,
    encode_grid_gain, encode_mesh_gain, process_gain, decode_grid_gain, decode_mesh_gain,
    encode_query, encode_keyval, encode_out, process_qkv, process_out,
    decode_query, decode_keyval, decode_out,
):
    hbm = pl.BlockSpec(memory_space=pl.ANY)
    vmem = pl.BlockSpec(memory_space=pltpu.VMEM)
    slabs = pltpu.VMEM((DEVICES, 16, 256), BF)
    rows = pltpu.VMEM((ROWS, D), BF)
    return pl.pallas_call(
        kernel,
        out_shape=jax.ShapeDtypeStruct((ROWS, D), BF),
        in_specs=[hbm, hbm, vmem, vmem, vmem] + [vmem] * 5 + [hbm] * 8,
        out_specs=vmem,
        scratch_shapes=[
            rows, rows,
            pltpu.VMEM((D, D), BF), pltpu.VMEM((D, 2 * D), BF), pltpu.VMEM((D, D), BF),
            pltpu.VMEM((D, 3 * D), BF), pltpu.VMEM((D, D), BF), pltpu.VMEM((D, D), BF),
            pltpu.VMEM((D, 2 * D), BF), pltpu.VMEM((D, D), BF),
            slabs, slabs, slabs, slabs, slabs, slabs,
            pltpu.VMEM((DEVICES, PAIR), F32),
            pltpu.VMEM((DEVICES, 1, PAIR), F32), pltpu.VMEM((DEVICES, 1, PAIR), F32),
            rows, rows, rows, rows,
            pltpu.VMEM((3 * ROWS, D), BF), pltpu.VMEM((SLOTS, D), BF),
            pltpu.VMEM((SLOTS, 2 * D), BF),
            pltpu.VMEM((SLOTS, PAIR), BF), pltpu.VMEM((SLOTS, PAIR), BF),
            pltpu.SemaphoreType.DMA((10,)), pltpu.SemaphoreType.DMA((4,)),
            pltpu.SemaphoreType.DMA((11,)), pltpu.SemaphoreType.DMA((8,)),
        ],
        compiler_params=pltpu.CompilerParams(
            collective_id=0, has_side_effects=True, vmem_limit_bytes=60 * 1024 * 1024
        ),
    )(
        grid_state, mesh_state, encode_block.reshape(1, -1), decode_block.reshape(1, -1),
        neighbour_block.reshape(1, -1),
        *(
            gain.reshape(1, -1)
            for gain in (
                encode_grid_gain, encode_mesh_gain, process_gain, decode_grid_gain, decode_mesh_gain,
            )
        ),
        encode_query, encode_keyval, encode_out, process_qkv, process_out,
        decode_query, decode_keyval, decode_out,
    )


def solution(mesh):
    rows, split = P(("gx", "gy"), None), P(("gx", "gy"))
    return jax.shard_map(
        on_device,
        mesh=mesh,
        in_specs=(rows, rows, split, split, split) + (P(),) * 13,
        out_specs=rows,
        check_vma=False,
    )
```

time: 98.2 us -> 90.1 us (0.918)
  Pallas kernels: 94.8 us -> 88 us
  local copies, waits for them, and re-layouts: 3.15 us -> 1.87 us
    pallas_call x1, Pallas kernels: 94.8 us -> 88 us  [on_device(): pl.pallas_call(kernel, out_shape=jax.ShapeDtypeStruct((ROWS, D), BF), in_...]
    broadcast_in_dim x1 -> x0, local copies, waits for them, and re-layouts: 1.28 us -> none  [on_device(): jnp.broadcast_to(neighbour_block[:, None], (2, PAIR))]
where the time goes in v1:
time: 90.1 us; the launch traced here: 89.9 us
  Pallas kernels  88 us (98%)
  local copies, waits for them, and re-layouts  1.87 us (2%)
    pallas_call x1, Pallas kernels, on_device(): pl.pallas_call(kernel, out_shape=jax.ShapeDtypeStruct((ROWS, D), BF), in_...  88 us
    unnamed x1, local copies, waits for them, and re-layouts  1.87 us

profile of v1, /device:TPU:1, one launch (start us, length us, event | category | flops | bytes accessed | tf_op | source)
XLA Modules:
  0.0 89.9 jit_solution(739759405632911391)
XLA Ops:
  0.0 88.0 %shard_map.172 = bf16[256,1024]{1,0:T(8,128)(2,1)} custom-call(bf16[256,1024]{1,0:T(8,128)(2,1)} %grid_hbm.1, bf16[256,1024]{1,0:T(8,128)(2,1)} %mesh_hbm.1, s32[1,256]{1,0:T(1,128)} %bitcast.13, s32[1,256]{1,0:T(1,128)} %bitcast.14, s32[1,2]{1,0:T(1,128)} %bitcast.15, f32[1,1024]{1,0:T(1,128)} %bitcast.8, f32[1,1024]{1,0:T(1,128)} %bitcast.9, ...), custom_call_target="tpu_custom_call" | custom-call | tf_op jit(solution)/shard_map/pallas_call | solution.py:457
  88.0 1.9 %copy.20 = bf16[256,1024]{1,0:T(8,128)(2,1)} copy(bf16[256,1024]{1,0:T(8,128)(2,1)} %shard_map.172) | data formatting | bytes 1048576

commit v2 on v1

--- a/solution.py
+++ b/solution.py
@@ -27,18 +27,29 @@
     return lax.axis_index("gx"), gy // 8, lax.rem(gy // 2, 4), lax.rem(gy, 2)
 
 
-def device_at(z, x, y, c):
-    return lax.rem(z + 4, 4), lax.rem(x + 4, 4) * 8 + lax.rem(y + 4, 4) * 2 + lax.rem(c + 2, 2)
-
-
-def peer(k, sign):
+def each_peer(visit, core, first, last, sign):
     z, x, y, c = coordinates()
-    return device_at(
-        z + sign * lax.rem(k // 16, 4),
-        x + sign * lax.rem(k, 4),
-        y + sign * lax.rem(k // 4, 4),
-        c + sign * (k // 64),
-    )
+    columns = [lax.rem(x + i, 4) * 8 for i in range(4)]
+    lines = [lax.rem(y + i, 4) * 2 for i in range(4)]
+    side = c if core == 0 else 1 - c
+
+    def plane(kz, start):
+        gx = lax.rem(z + sign * kz + 4, 4)
+        for ky in range(4):
+            line = lines[sign * ky % 4] + side
+            for kx in range(4):
+                if kx + 4 * ky >= start:
+                    visit(64 * core + 16 * kz + 4 * ky + kx, (gx, columns[sign * kx % 4] + line))
+
+    if core == 0 and first == 0:
+        plane(0, 1)
+        first = 1
+
+    def step(kz, carry):
+        plane(kz, 0)
+        return carry
+
+    lax.fori_loop(first, last, step, 0)
 
 
 def iota(shape, dim):
@@ -120,13 +131,11 @@
     return jnp.concatenate([tall[64 * q : 64 * q + 64] for q in range(4)], axis=1)
 
 
-def pack(rows_ref, slot, dst, mix, first, last):
-    def step(j, carry):
-        chosen = ones_where(iota((64, ROWS), 0) + 64 * j == slot)
-        store_slabs(dst, j, matmul(chosen, rows_ref[...]).astype(BF), mix)
-        return carry
-
-    lax.fori_loop(first, last, step, 0)
+def pack(rows_ref, slot, dst, mix, half):
+    chosen = ones_where(iota((ROWS, ROWS), 0) + ROWS * half == slot)
+    rows = matmul(chosen, rows_ref[...]).astype(BF)
+    for j in range(4):
+        store_slabs(dst, 4 * half + j, rows[64 * j : 64 * j + 64], mix)
 
 
 def unpack(src, dst, unmix, first, last):
@@ -134,7 +143,7 @@
         dst[pl.ds(pl.multiple_of(64 * j, 64), 64), :] = load_slabs(src, j, unmix)
         return carry
 
-    lax.fori_loop(first, last, step, 0)
+    lax.fori_loop(first, last, step, 0, unroll=True)
 
 
 def attend_pairs(pairs):
@@ -171,9 +180,8 @@
     me = lax.axis_index("gx") * 32 + lax.axis_index("gy")
     barrier = pltpu.get_barrier_semaphore()
 
-    def greet(k, carry):
-        pl.semaphore_signal(barrier, inc=1, device_id=peer(k, 1), device_id_type=MESH)
-        return carry
+    def greet(k, device):
+        pl.semaphore_signal(barrier, inc=1, device_id=device, device_id_type=MESH)
 
     loads = [
         pltpu.make_async_copy(src, dst, load_sems.at[i])
@@ -185,22 +193,19 @@
         )
     ]
     loads[0].start()
-    lax.fori_loop(1, DEVICES, greet, 0)
+    each_peer(greet, 0, 0, 4, 1)
+    each_peer(greet, 1, 0, 4, 1)
     for load in loads[1:]:
         load.start()
 
-    def remote(src, dst, sent, received, k, sign):
-        return pltpu.make_async_remote_copy(
-            src_ref=src.at[k], dst_ref=dst.at[k], send_sem=send_sems.at[sent],
-            recv_sem=recv_sems.at[received], device_id=peer(k, sign), device_id_type=MESH,
-        )
-
-    def send_range(src, dst, sent, received, first, last, sign):
-        def send(k, carry):
-            remote(src, dst, sent, received, k, sign).start()
-            return carry
-
-        lax.fori_loop(max(1, first), last, send, 0)
+    def send_planes(src, dst, sent, received, core, first, last, sign):
+        def send(k, device):
+            pltpu.make_async_remote_copy(
+                src_ref=src.at[k], dst_ref=dst.at[k], send_sem=send_sems.at[sent],
+                recv_sem=recv_sems.at[received], device_id=device, device_id_type=MESH,
+            ).start()
+
+        each_peer(send, core, first, last, sign)
 
     def wait_for(ref, first, last, sem):
         view = ref.at[pl.ds(max(1, first), last - max(1, first))]
@@ -210,11 +215,11 @@
     e_matches, e_rank, e_slot = slot_plan(encode_block[...])
     loads[0].wait()
     norm_into(grid, 0, rows_a, 0, encode_grid_gain)
-    pack(rows_a, e_slot, send1, mix, 0, 4)
+    pack(rows_a, e_slot, send1, mix, 0)
     pl.semaphore_wait(barrier, DEVICES - 1)
-    send_range(send1, recv1, 0, 0, 0, 64, 1)
-    pack(rows_a, e_slot, send1, mix, 4, 8)
-    send_range(send1, recv1, 0, 1, 64, 128, 1)
+    send_planes(send1, recv1, 0, 0, 0, 0, 4, 1)
+    pack(rows_a, e_slot, send1, mix, 1)
+    send_planes(send1, recv1, 0, 1, 1, 0, 4, 1)
 
     d_matches, d_rank, d_slot = slot_plan(decode_block[...])
     lab2d[...] = label_table(e_matches, e_rank, encode_block[...], 0) + label_table(
@@ -225,9 +230,10 @@
         lab_send[k] = lab2d[pl.ds(k, 1), :]
         return carry
 
-    lax.fori_loop(0, DEVICES, spread, 0)
+    lax.fori_loop(0, DEVICES, spread, 0, unroll=8)
     norm_into(grid, 0, rows_a, 0, decode_grid_gain)
-    send_range(lab_send, lab_recv, 1, 2, 0, 128, 1)
+    for core in range(2):
+        send_planes(lab_send, lab_recv, 1, 2, core, 0, 4, 1)
 
     loads[1].wait()
 
@@ -235,9 +241,10 @@
         rows_b[:, at] = (out * SCORE_SCALE).astype(BF)
 
     project(rows_a, dq, D, 0, store_query)
-    pack(rows_b, d_slot, send2, mix, 0, 8)
+    pack(rows_b, d_slot, send2, mix, 0)
     for group in range(2):
-        send_range(send2, recv2, 2, 3 + group, 32 * group, 32 * group + 32, 1)
+        send_planes(send2, recv2, 2, 3 + group, 0, 2 * group, 2 * group + 2, 1)
+    pack(rows_b, d_slot, send2, mix, 1)
 
     loads[2].wait()
     norm_into(mesh, 0, rows_a, 0, encode_mesh_gain)
@@ -267,7 +274,7 @@
         lab2d[pl.ds(k, 1), :] = lab_recv[k]
         return carry
 
-    lax.fori_loop(0, DEVICES, gather_labels, 0)
+    lax.fori_loop(0, DEVICES, gather_labels, 0, unroll=8)
     spread_rows = matmul(
         ones_where((iota((SLOTS, DEVICES), 0) >> 2) == iota((SLOTS, DEVICES), 1)),
         lab2d[...].astype(BF),
@@ -328,8 +335,8 @@
         for step, sem, to in ((1, 4 * block, 0), (-1, 4 * block + 2, 2 * ROWS)):
             halos.append(halo(block, step, sem, to))
             halos[-1].start()
-    for group in range(2, 4):
-        send_range(send2, recv2, 2, 3 + group, 32 * group, 32 * group + 32, 1)
+    for group in range(2):
+        send_planes(send2, recv2, 2, 5 + group, 1, 2 * group, 2 * group + 2, 1)
 
     loads[6].wait()
 
@@ -415,7 +422,7 @@
         lax.fori_loop(0, 2, decode_pairs, 0)
         for j in range(2):
             store_slabs(send3, 2 * chunk + j, rows_a[pl.ds(64 * j, 64), :], mix)
-        send_range(send3, recv3, 3, 7 + chunk, 32 * chunk, 32 * chunk + 32, -1)
+        send_planes(send3, recv3, 3, 7 + chunk, chunk // 2, chunk % 2 * 2, chunk % 2 * 2 + 2, -1)
     recv3[0] = send3[0]
     slot_column = jnp.sum(
         jnp.where(iota((ROWS, ROWS), 0) == iota((ROWS, ROWS), 1), d_slot, 0).astype(F32),

time: 90.1 us -> 77.6 us (0.86)
  Pallas kernels: 88 us -> 75.5 us
    pallas_call x1, Pallas kernels: 88 us -> 75.5 us  [on_device(): pl.pallas_call(kernel, out_shape=jax.ShapeDtypeStruct((ROWS, D), BF), in_...]
where the time goes in v2:
time: 77.6 us; the launch traced here: 77.4 us
  Pallas kernels  75.5 us (97%)
  local copies, waits for them, and re-layouts  1.87 us (2%)
    pallas_call x1, Pallas kernels, on_device(): pl.pallas_call(kernel, out_shape=jax.ShapeDtypeStruct((ROWS, D), BF), in_...  75.5 us
    unnamed x1, local copies, waits for them, and re-layouts  1.87 us

profile of v2, /device:TPU:1, one launch (start us, length us, event | category | flops | bytes accessed | tf_op | source)
XLA Modules:
  0.0 77.4 jit_solution(1759719229596589028)
XLA Ops:
  0.0 75.5 %shard_map.172 = bf16[256,1024]{1,0:T(8,128)(2,1)} custom-call(bf16[256,1024]{1,0:T(8,128)(2,1)} %grid_hbm.1, bf16[256,1024]{1,0:T(8,128)(2,1)} %mesh_hbm.1, s32[1,256]{1,0:T(1,128)} %bitcast.13, s32[1,256]{1,0:T(1,128)} %bitcast.14, s32[1,2]{1,0:T(1,128)} %bitcast.15, f32[1,1024]{1,0:T(1,128)} %bitcast.8, f32[1,1024]{1,0:T(1,128)} %bitcast.9, ...), custom_call_target="tpu_custom_call" | custom-call | tf_op jit(solution)/shard_map/pallas_call | solution.py:464
  75.5 1.9 %copy.20 = bf16[256,1024]{1,0:T(8,128)(2,1)} copy(bf16[256,1024]{1,0:T(8,128)(2,1)} %shard_map.172) | data formatting | bytes 1048576

commit v3 on v2

--- a/solution.py
+++ b/solution.py
@@ -87,7 +87,7 @@
         epilogue(pl.ds(at, tile), out)
         return carry
 
-    lax.fori_loop(0, columns // tile, step, 0)
+    lax.fori_loop(0, columns // tile, step, 0, unroll=True)
 
 
 def slot_plan(blocks):
@@ -242,8 +242,6 @@
 
     project(rows_a, dq, D, 0, store_query)
     pack(rows_b, d_slot, send2, mix, 0)
-    for group in range(2):
-        send_planes(send2, recv2, 2, 3 + group, 0, 2 * group, 2 * group + 2, 1)
     pack(rows_b, d_slot, send2, mix, 1)
 
     loads[2].wait()
@@ -293,6 +291,8 @@
     query_tags[...] = slot_tags(CAP)
 
     def pair_at(p):
+        if isinstance(p, int):
+            return pl.ds(p * PAIR, PAIR), pl.ds(D + p * PAIR, PAIR)
         return (
             pl.ds(pl.multiple_of(p * PAIR, PAIR), PAIR),
             pl.ds(pl.multiple_of(D + p * PAIR, PAIR), PAIR),
@@ -307,25 +307,25 @@
             device_id=(there // 32, lax.rem(there, 32)), device_id_type=MESH,
         )
 
+    node_tag = ones_where(iota((ROWS, PAIR), 1) == (iota((ROWS, PAIR), 0) >> 7))
+
+    def encode_pairs(g, carry):
+        spots = [pair_at(4 * g + i) for i in range(4)]
+        outs = attend_pairs(
+            [
+                (query[:, at], node_tag, keyval[:, at], key_tags[...], keyval[:, upper])
+                for at, upper in spots
+            ]
+        )
+        for (at, _), out in zip(spots, outs):
+            rows_a[:, at] = out
+        return carry
+
+    lax.fori_loop(0, 2, encode_pairs, 0)
     halos = []
     loads[5].wait()
     for block in range(2):
         here = pl.ds(block * BLOCK, BLOCK)
-        block_tag = ones_where(iota((BLOCK, PAIR), 1) == block)
-
-        def encode_pairs(g, carry):
-            spots = [pair_at(4 * g + i) for i in range(4)]
-            outs = attend_pairs(
-                [
-                    (query[here, at], block_tag, keyval[:, at], key_tags[...], keyval[:, upper])
-                    for at, upper in spots
-                ]
-            )
-            for (at, _), out in zip(spots, outs):
-                rows_a[here, at] = out
-            return carry
-
-        lax.fori_loop(0, 2, encode_pairs, 0)
 
         def store_mid(at, out):
             mid[here, at] = (mesh[here, at].astype(F32) + out).astype(BF)
@@ -335,8 +335,10 @@
         for step, sem, to in ((1, 4 * block, 0), (-1, 4 * block + 2, 2 * ROWS)):
             halos.append(halo(block, step, sem, to))
             halos[-1].start()
-    for group in range(2):
-        send_planes(send2, recv2, 2, 5 + group, 1, 2 * group, 2 * group + 2, 1)
+    for group in range(4):
+        send_planes(
+            send2, recv2, 2, 3 + group, group // 2, group % 2 * 2, group % 2 * 2 + 2, 1
+        )
 
     loads[6].wait()
 
@@ -370,7 +372,7 @@
     project(rows_b, pqkv, 2 * D, D, store_other)
 
     def process_pairs(g, carry):
-        spots = [(block, *pair_at(2 * g + i)) for i in range(2) for block in range(2)]
+        spots = [(block, *pair_at(4 * g + i)) for i in range(4) for block in range(2)]
         work = []
         for block, at, upper in spots:
             here = pl.ds(block * BLOCK, BLOCK)
@@ -386,7 +388,7 @@
             rows_a[pl.ds(block * BLOCK, BLOCK), at] = out
         return carry
 
-    lax.fori_loop(0, HEADS // 4, process_pairs, 0)
+    lax.fori_loop(0, 2, process_pairs, 0)
     loads[7].wait()
 
     def store_mesh_out(at, out):
@@ -397,29 +399,24 @@
     loads[8].wait()
     project(rows_a, dkv, 2 * D, 0, store_own)
 
-    node_tag = ones_where(iota((ROWS, PAIR), 1) == (iota((ROWS, PAIR), 0) >> 7))
     mine = pl.ds(0, ROWS)
     for chunk in range(4):
         here = pl.ds(chunk * BLOCK, BLOCK)
         wait_for(recv2, 32 * chunk, 32 * chunk + 32, recv_sems.at[3 + chunk])
         unpack(recv2, wide_rows, unmix, 2 * chunk, 2 * chunk + 2)
 
-        def decode_pairs(g, carry):
-            spots = [pair_at(4 * g + i) for i in range(4)]
-            outs = attend_pairs(
-                [
-                    (
-                        wide_rows[here, at], query_tags[here, :],
-                        keyval[mine, at], node_tag, keyval[mine, upper],
-                    )
-                    for at, upper in spots
-                ]
-            )
-            for (at, _), out in zip(spots, outs):
-                rows_a[pl.ds(0, BLOCK), at] = out
-            return carry
-
-        lax.fori_loop(0, 2, decode_pairs, 0)
+        spots = [pair_at(i) for i in range(8)]
+        outs = attend_pairs(
+            [
+                (
+                    wide_rows[here, at], query_tags[here, :],
+                    keyval[mine, at], node_tag, keyval[mine, upper],
+                )
+                for at, upper in spots
+            ]
+        )
+        for (at, _), out in zip(spots, outs):
+            rows_a[pl.ds(0, BLOCK), at] = out
         for j in range(2):
             store_slabs(send3, 2 * chunk + j, rows_a[pl.ds(64 * j, 64), :], mix)
         send_planes(send3, recv3, 3, 7 + chunk, chunk // 2, chunk % 2 * 2, chunk % 2 * 2 + 2, -1)

time: 77.6 us -> 79.6 us (1.026)
  Pallas kernels: 75.5 us -> 77.6 us
    pallas_call x1, Pallas kernels: 75.5 us -> 77.6 us  [on_device(): pl.pallas_call(kernel, out_shape=jax.ShapeDtypeStruct((ROWS, D), BF), in_...]
where the time goes in v3:
time: 79.6 us; the launch traced here: 79.5 us
  Pallas kernels  77.6 us (97%)
  local copies, waits for them, and re-layouts  1.87 us (2%)
    pallas_call x1, Pallas kernels, on_device(): pl.pallas_call(kernel, out_shape=jax.ShapeDtypeStruct((ROWS, D), BF), in_...  77.6 us
    unnamed x1, local copies, waits for them, and re-layouts  1.87 us

profile of v3, /device:TPU:1, one launch (start us, length us, event | category | flops | bytes accessed | tf_op | source)
XLA Modules:
  0.0 79.5 jit_solution(5192259315089999491)
XLA Ops:
  0.0 77.6 %shard_map.172 = bf16[256,1024]{1,0:T(8,128)(2,1)} custom-call(bf16[256,1024]{1,0:T(8,128)(2,1)} %grid_hbm.1, bf16[256,1024]{1,0:T(8,128)(2,1)} %mesh_hbm.1, s32[1,256]{1,0:T(1,128)} %bitcast.13, s32[1,256]{1,0:T(1,128)} %bitcast.14, s32[1,2]{1,0:T(1,128)} %bitcast.15, f32[1,1024]{1,0:T(1,128)} %bitcast.8, f32[1,1024]{1,0:T(1,128)} %bitcast.9, ...), custom_call_target="tpu_custom_call" | custom-call | tf_op jit(solution)/shard_map/pallas_call | solution.py:461
  77.6 1.9 %copy.20 = bf16[256,1024]{1,0:T(8,128)(2,1)} copy(bf16[256,1024]{1,0:T(8,128)(2,1)} %shard_map.172) | data formatting | bytes 1048576

commit v4 on v3

--- a/solution.py
+++ b/solution.py
@@ -218,9 +218,6 @@
     pack(rows_a, e_slot, send1, mix, 0)
     pl.semaphore_wait(barrier, DEVICES - 1)
     send_planes(send1, recv1, 0, 0, 0, 0, 4, 1)
-    pack(rows_a, e_slot, send1, mix, 1)
-    send_planes(send1, recv1, 0, 1, 1, 0, 4, 1)
-
     d_matches, d_rank, d_slot = slot_plan(decode_block[...])
     lab2d[...] = label_table(e_matches, e_rank, encode_block[...], 0) + label_table(
         d_matches, d_rank, decode_block[...], CAP
@@ -231,9 +228,12 @@
         return carry
 
     lax.fori_loop(0, DEVICES, spread, 0, unroll=8)
-    norm_into(grid, 0, rows_a, 0, decode_grid_gain)
     for core in range(2):
         send_planes(lab_send, lab_recv, 1, 2, core, 0, 4, 1)
+    pack(rows_a, e_slot, send1, mix, 1)
+    send_planes(send1, recv1, 0, 1, 1, 0, 4, 1)
+
+    norm_into(grid, 0, rows_a, 0, decode_grid_gain)
 
     loads[1].wait()
 
@@ -242,6 +242,8 @@
 
     project(rows_a, dq, D, 0, store_query)
     pack(rows_b, d_slot, send2, mix, 0)
+    for group in range(2):
+        send_planes(send2, recv2, 2, 3 + group, 0, 2 * group, 2 * group + 2, 1)
     pack(rows_b, d_slot, send2, mix, 1)
 
     loads[2].wait()
@@ -256,7 +258,7 @@
     recv2[0] = send2[0]
     lab_recv[0] = lab_send[0]
     loads[4].wait()
-    for group in range(2):
+    def key_values(group):
         wait_for(recv1, 64 * group, 64 * group + 64, recv_sems.at[group])
         unpack(recv1, wide_rows, unmix, 4 * group, 4 * group + 4)
         part = pl.ds(group * ROWS, ROWS)
@@ -266,6 +268,7 @@
 
         project(wide_rows.at[part], ekv, 2 * D, 0, store_keyval)
 
+    key_values(0)
     wait_for(lab_recv, 0, DEVICES, recv_sems.at[2])
 
     def gather_labels(k, carry):
@@ -290,6 +293,8 @@
     key_tags[...] = slot_tags(0)
     query_tags[...] = slot_tags(CAP)
 
+    key_values(1)
+
     def pair_at(p):
         if isinstance(p, int):
             return pl.ds(p * PAIR, PAIR), pl.ds(D + p * PAIR, PAIR)
@@ -335,10 +340,8 @@
         for step, sem, to in ((1, 4 * block, 0), (-1, 4 * block + 2, 2 * ROWS)):
             halos.append(halo(block, step, sem, to))
             halos[-1].start()
-    for group in range(4):
-        send_planes(
-            send2, recv2, 2, 3 + group, group // 2, group % 2 * 2, group % 2 * 2 + 2, 1
-        )
+    for group in range(2):
+        send_planes(send2, recv2, 2, 5 + group, 1, 2 * group, 2 * group + 2, 1)
 
     loads[6].wait()
 

time: 79.6 us -> 74.3 us (0.933)
  Pallas kernels: 77.6 us -> 72.2 us
    pallas_call x1, Pallas kernels: 77.6 us -> 72.2 us  [on_device(): pl.pallas_call(kernel, out_shape=jax.ShapeDtypeStruct((ROWS, D), BF), in_...]
where the time goes in v4:
time: 74.3 us; the launch traced here: 74.1 us
  Pallas kernels  72.2 us (97%)
  local copies, waits for them, and re-layouts  1.87 us (3%)
    pallas_call x1, Pallas kernels, on_device(): pl.pallas_call(kernel, out_shape=jax.ShapeDtypeStruct((ROWS, D), BF), in_...  72.2 us
    unnamed x1, local copies, waits for them, and re-layouts  1.87 us

profile of v4, /device:TPU:1, one launch (start us, length us, event | category | flops | bytes accessed | tf_op | source)
XLA Modules:
  0.0 74.1 jit_solution(9466809202385671197)
XLA Ops:
  0.0 72.2 %shard_map.172 = bf16[256,1024]{1,0:T(8,128)(2,1)} custom-call(bf16[256,1024]{1,0:T(8,128)(2,1)} %grid_hbm.1, bf16[256,1024]{1,0:T(8,128)(2,1)} %mesh_hbm.1, s32[1,256]{1,0:T(1,128)} %bitcast.13, s32[1,256]{1,0:T(1,128)} %bitcast.14, s32[1,2]{1,0:T(1,128)} %bitcast.15, f32[1,1024]{1,0:T(1,128)} %bitcast.8, f32[1,1024]{1,0:T(1,128)} %bitcast.9, ...), custom_call_target="tpu_custom_call" | custom-call | tf_op jit(solution)/shard_map/pallas_call | solution.py:464
  72.2 1.9 %copy.20 = bf16[256,1024]{1,0:T(8,128)(2,1)} copy(bf16[256,1024]{1,0:T(8,128)(2,1)} %shard_map.172) | data formatting | bytes 1048576

commit v5 on v4

--- a/solution.py
+++ b/solution.py
@@ -167,10 +167,10 @@
 
 
 def kernel(
-    grid_hbm, mesh_hbm, encode_block, decode_block, neighbour_block,
+    grid_hbm, mesh_hbm, eb_hbm, db_hbm, nb_hbm, eg_hbm, em_hbm, pg_hbm, dg_hbm, dm_hbm, eq_hbm, ekv_hbm, eo_hbm, pqkv_hbm, po_hbm, dq_hbm, dkv_hbm, do_hbm,
+    out_ref,
+    encode_block, decode_block, neighbour_block,
     encode_grid_gain, encode_mesh_gain, process_gain, decode_grid_gain, decode_mesh_gain,
-    eq_hbm, ekv_hbm, eo_hbm, pqkv_hbm, po_hbm, dq_hbm, dkv_hbm, do_hbm,
-    out_ref,
     grid, mesh, eq, ekv, eo, pqkv, po, dq, dkv, do,
     send1, recv1, send2, recv2, send3, recv3, lab2d, lab_send, lab_recv,
     rows_a, rows_b, query, mid, cand, wide_rows, keyval, key_tags, query_tags,
@@ -192,7 +192,19 @@
             )
         )
     ]
+    small = [
+        pltpu.make_async_copy(src, dst, load_sems.at[10 + i])
+        for i, (src, dst) in enumerate(
+            (
+                (eb_hbm, encode_block), (db_hbm, decode_block), (nb_hbm, neighbour_block),
+                (eg_hbm, encode_grid_gain), (em_hbm, encode_mesh_gain), (pg_hbm, process_gain),
+                (dg_hbm, decode_grid_gain), (dm_hbm, decode_mesh_gain),
+            )
+        )
+    ]
     loads[0].start()
+    for load in small:
+        load.start()
     each_peer(greet, 0, 0, 4, 1)
     each_peer(greet, 1, 0, 4, 1)
     for load in loads[1:]:
@@ -212,6 +224,8 @@
         pltpu.make_async_copy(view, view, sem).wait()
 
     mix, unmix = interleave(), separate()
+    for load in small:
+        load.wait()
     e_matches, e_rank, e_slot = slot_plan(encode_block[...])
     loads[0].wait()
     norm_into(grid, 0, rows_a, 0, encode_grid_gain)
@@ -461,12 +475,14 @@
     vmem = pl.BlockSpec(memory_space=pltpu.VMEM)
     slabs = pltpu.VMEM((DEVICES, 16, 256), BF)
     rows = pltpu.VMEM((ROWS, D), BF)
+    ids, gain = pltpu.VMEM((1, ROWS), jnp.int32), pltpu.VMEM((1, D), F32)
     return pl.pallas_call(
         kernel,
         out_shape=jax.ShapeDtypeStruct((ROWS, D), BF),
-        in_specs=[hbm, hbm, vmem, vmem, vmem] + [vmem] * 5 + [hbm] * 8,
+        in_specs=[hbm] * 18,
         out_specs=vmem,
         scratch_shapes=[
+            ids, ids, pltpu.VMEM((1, 2), jnp.int32), gain, gain, gain, gain, gain,
             rows, rows,
             pltpu.VMEM((D, D), BF), pltpu.VMEM((D, 2 * D), BF), pltpu.VMEM((D, D), BF),
             pltpu.VMEM((D, 3 * D), BF), pltpu.VMEM((D, D), BF), pltpu.VMEM((D, D), BF),
@@ -478,7 +494,7 @@
             pltpu.VMEM((3 * ROWS, D), BF), pltpu.VMEM((SLOTS, D), BF),
             pltpu.VMEM((SLOTS, 2 * D), BF),
             pltpu.VMEM((SLOTS, PAIR), BF), pltpu.VMEM((SLOTS, PAIR), BF),
-            pltpu.SemaphoreType.DMA((10,)), pltpu.SemaphoreType.DMA((4,)),
+            pltpu.SemaphoreType.DMA((18,)), pltpu.SemaphoreType.DMA((4,)),
             pltpu.SemaphoreType.DMA((11,)), pltpu.SemaphoreType.DMA((8,)),
         ],
         compiler_params=pltpu.CompilerParams(
@@ -488,8 +504,8 @@
         grid_state, mesh_state, encode_block.reshape(1, -1), decode_block.reshape(1, -1),
         neighbour_block.reshape(1, -1),
         *(
-            gain.reshape(1, -1)
-            for gain in (
+            value.reshape(1, -1)
+            for value in (
                 encode_grid_gain, encode_mesh_gain, process_gain, decode_grid_gain, decode_mesh_gain,
             )
         ),

time: 74.3 us -> 73.6 us (level)
  no operation moved by 1% of the time
where the time goes in v5:
time: 73.6 us; the launch traced here: 73.5 us
  Pallas kernels  71.6 us (97%)
  local copies, waits for them, and re-layouts  1.87 us (3%)
    pallas_call x1, Pallas kernels, on_device(): pl.pallas_call(kernel, out_shape=jax.ShapeDtypeStruct((ROWS, D), BF), in_...  71.6 us
    unnamed x1, local copies, waits for them, and re-layouts  1.87 us

profile of v5, /device:TPU:1, one launch (start us, length us, event | category | flops | bytes accessed | tf_op | source)
XLA Modules:
  0.0 73.5 jit_solution(4438422955299204626)
XLA Ops:
  0.0 71.6 %shard_map.172 = bf16[256,1024]{1,0:T(8,128)(2,1)} custom-call(bf16[256,1024]{1,0:T(8,128)(2,1)} %grid_hbm.1, bf16[256,1024]{1,0:T(8,128)(2,1)} %mesh_hbm.1, s32[1,256]{1,0:T(1,128)} %bitcast.13, s32[1,256]{1,0:T(1,128)} %bitcast.14, s32[1,2]{1,0:T(1,128)} %bitcast.15, f32[1,1024]{1,0:T(1,128)} %bitcast.8, f32[1,1024]{1,0:T(1,128)} %bitcast.9, ...), custom_call_target="tpu_custom_call" | custom-call | tf_op jit(solution)/shard_map/pallas_call | solution.py:479
  71.6 1.9 %copy.20 = bf16[256,1024]{1,0:T(8,128)(2,1)} copy(bf16[256,1024]{1,0:T(8,128)(2,1)} %shard_map.172) | data formatting | bytes 1048576

commit v6 on v5

--- a/solution.py
+++ b/solution.py
@@ -259,6 +259,7 @@
     for group in range(2):
         send_planes(send2, recv2, 2, 3 + group, 0, 2 * group, 2 * group + 2, 1)
     pack(rows_b, d_slot, send2, mix, 1)
+    send_planes(send2, recv2, 2, 5, 1, 0, 1, 1)
 
     loads[2].wait()
     norm_into(mesh, 0, rows_a, 0, encode_mesh_gain)
@@ -354,8 +355,8 @@
         for step, sem, to in ((1, 4 * block, 0), (-1, 4 * block + 2, 2 * ROWS)):
             halos.append(halo(block, step, sem, to))
             halos[-1].start()
-    for group in range(2):
-        send_planes(send2, recv2, 2, 5 + group, 1, 2 * group, 2 * group + 2, 1)
+    send_planes(send2, recv2, 2, 5, 1, 1, 2, 1)
+    send_planes(send2, recv2, 2, 6, 1, 2, 4, 1)
 
     loads[6].wait()
 
@@ -446,22 +447,23 @@
     wait_for(send1, 0, DEVICES, send_sems.at[0])
     wait_for(lab_send, 0, DEVICES, send_sems.at[1])
     wait_for(send2, 0, DEVICES, send_sems.at[2])
-    decoded = None
+    loads[9].wait()
+    update = None
+    some = pl.ds(0, BLOCK)
+
+    def store_projected(at, out):
+        rows_a[some, at] = out.astype(BF)
+
     for chunk in range(4):
         choose = ones_where(
             (iota((ROWS, BLOCK), 1) + chunk * BLOCK).astype(F32) == slot_column
         )
         wait_for(recv3, 32 * chunk, 32 * chunk + 32, recv_sems.at[7 + chunk])
         unpack(recv3, wide_rows, unmix, 2 * chunk, 2 * chunk + 2)
-        found = matmul(choose, wide_rows[pl.ds(chunk * BLOCK, BLOCK), :])
-        decoded = found if decoded is None else decoded + found
-    rows_b[...] = decoded.astype(BF)
-    loads[9].wait()
-
-    def store_out(at, out):
-        out_ref[:, at] = out.astype(BF)
-
-    project(rows_b, do, D, 0, store_out)
+        project(wide_rows.at[pl.ds(chunk * BLOCK, BLOCK)], do, D, 0, store_projected)
+        found = matmul(choose, rows_a[some, :])
+        update = found if update is None else update + found
+    out_ref[...] = update.astype(BF)
     wait_for(send3, 0, DEVICES, send_sems.at[3])
 
 

time: 73.6 us -> 72 us (0.978)
  Pallas kernels: 71.6 us -> 70 us
    pallas_call x1, Pallas kernels: 71.6 us -> 70 us  [on_device(): pl.pallas_call(kernel, out_shape=jax.ShapeDtypeStruct((ROWS, D), BF), in_...]
where the time goes in v6:
time: 72 us; the launch traced here: 71.8 us
  Pallas kernels  70 us (97%)
  local copies, waits for them, and re-layouts  1.87 us (3%)
    pallas_call x1, Pallas kernels, on_device(): pl.pallas_call(kernel, out_shape=jax.ShapeDtypeStruct((ROWS, D), BF), in_...  70 us
    unnamed x1, local copies, waits for them, and re-layouts  1.87 us

profile of v6, /device:TPU:1, one launch (start us, length us, event | category | flops | bytes accessed | tf_op | source)
XLA Modules:
  0.0 71.8 jit_solution(9999976166016203036)
XLA Ops:
  0.0 70.0 %shard_map.172 = bf16[256,1024]{1,0:T(8,128)(2,1)} custom-call(bf16[256,1024]{1,0:T(8,128)(2,1)} %grid_hbm.1, bf16[256,1024]{1,0:T(8,128)(2,1)} %mesh_hbm.1, s32[1,256]{1,0:T(1,128)} %bitcast.13, s32[1,256]{1,0:T(1,128)} %bitcast.14, s32[1,2]{1,0:T(1,128)} %bitcast.15, f32[1,1024]{1,0:T(1,128)} %bitcast.8, f32[1,1024]{1,0:T(1,128)} %bitcast.9, ...), custom_call_target="tpu_custom_call" | custom-call | tf_op jit(solution)/shard_map/pallas_call | solution.py:481
  70.0 1.9 %copy.20 = bf16[256,1024]{1,0:T(8,128)(2,1)} copy(bf16[256,1024]{1,0:T(8,128)(2,1)} %shard_map.172) | data formatting | bytes 1048576
